TPU v7x, 32 devices: a whole 2x2x4 slice. The times are simulated.
32 devices in a mesh: dp: 4 (over x, core), ctx: 4 (over z), tensor: 2 (over y).
Axes of the slice: x: 2, y: 2, z: 4, core: 2. Of those that a mesh axis runs over, the one named last changes fastest.
Arguments:
- block_in: bfloat16 [8, 512, 2048], P('dp', 'ctx'), may hold values from -8 to 8
- attn_gain: bfloat16 [2048], replicated, may hold values from 0.5 to 1.5
- query_weight: bfloat16 [2048, 2048], P(None, 'tensor'), may hold values from -1 to 1
- key_weight: bfloat16 [2048, 512], P(None, 'tensor'), may hold values from -1 to 1
- value_weight: bfloat16 [2048, 512], P(None, 'tensor'), may hold values from -0.125 to 0.125
- output_weight: bfloat16 [2048, 2048], P('tensor'), may hold values from -0.75 to 0.75
- mlp_gain: bfloat16 [2048], replicated, may hold values from 0.5 to 1.5
- gate_weight: bfloat16 [2048, 8192], P(None, 'tensor'), may hold values from -0.125 to 0.125
- up_weight: bfloat16 [2048, 8192], P(None, 'tensor'), may hold values from -0.125 to 0.125
- down_weight: bfloat16 [8192, 2048], P('tensor'), may hold values from -0.0625 to 0.0625
- cotangent: bfloat16 [8, 512, 2048], P('dp', 'ctx'), may hold values from -6 to 6
Outputs:
- block_out: bfloat16 [8, 512, 2048], P('dp', ('ctx', 'tensor'))
- input_grad: float32 [8, 512, 2048], P('dp', ('ctx', 'tensor'))
- grad_attn_gain: float32 [2048], P(('dp', 'ctx'))
- grad_query: float32 [2048, 2048], P(('dp', 'ctx'), 'tensor')
- grad_key: float32 [2048, 512], P(('dp', 'ctx'), 'tensor')
- grad_value: float32 [2048, 512], P(('dp', 'ctx'), 'tensor')
- grad_output: float32 [2048, 2048], P('tensor', ('dp', 'ctx'))
- grad_mlp_gain: float32 [2048], P(('dp', 'ctx'))
- grad_gate: float32 [2048, 8192], P(('dp', 'ctx'), 'tensor')
- grad_up: float32 [2048, 8192], P(('dp', 'ctx'), 'tensor')
- grad_down: float32 [8192, 2048], P('tensor', ('dp', 'ctx'))
All inputs are finite; a program needn't handle non-finite values.
Results may differ from a plain program's by a relative error of at most 0.024.
Values may be sent and summed in bfloat16 or wider, within the bound.
A program may use at most 256 MiB of HBM per device.

v0:
```python
import jax
import jax.numpy as jnp
from jax import lax
from jax.sharding import PartitionSpec as P

HD = 64


norm_eps = 1e-05
rope_base = 500000.0


def rms_apply(values, gain):
    return values * lax.rsqrt(jnp.mean(values * values, axis=-1, keepdims=True) + norm_eps) * gain


def gated(gate_input, up_input):
    return jax.nn.silu(gate_input) * up_input


def rope_tables(positions, head_size):
    half_width = head_size // 2
    frequency = rope_base ** (-jnp.arange(half_width, dtype=jnp.float32) * 2.0 / head_size)
    angles = positions.astype(jnp.float32)[:, None] * frequency[None, :]
    return (jnp.cos(angles)[:, None, :], jnp.sin(angles)[:, None, :])


def rotate(vectors, cosine, sine_table):
    half_width = vectors.shape[-1] // 2
    first_half = vectors[..., :half_width]
    second_half = vectors[..., half_width:]
    return jnp.concatenate(
        [
            first_half * cosine - second_half * sine_table,
            second_half * cosine + first_half * sine_table,
        ],
        axis=-1,
    )


def unrotate(gradient, cosine, sine_table):
    half_width = gradient.shape[-1] // 2
    first_half = gradient[..., :half_width]
    second_half = gradient[..., half_width:]
    return jnp.concatenate(
        [
            first_half * cosine + second_half * sine_table,
            second_half * cosine - first_half * sine_table,
        ],
        axis=-1,
    )


def rows_product(left, right):
    return lax.dot_general(
        left, right, (((0,), (0,)), ((), ())), preferred_element_type=jnp.float32
    )


def back_product(left, right):
    return lax.dot_general(
        left, right, (((1,), (1,)), ((), ())), preferred_element_type=jnp.float32
    )


def shards(
    block_in,
    attn_gain,
    query_weight,
    key_weight,
    value_weight,
    output_weight,
    mlp_gain,
    gate_weight,
    up_weight,
    down_weight,
    cotangent,
):
    seq_count, ctx_tok, model_width = block_in.shape
    tensor_ranks = lax.axis_size("tensor")
    share_len = ctx_tok // tensor_ranks
    share_start = lax.axis_index("tensor") * share_len
    row_count = seq_count * ctx_tok
    query_heads = query_weight.shape[1] // HD
    key_heads = key_weight.shape[1] // HD
    group_size = query_heads // key_heads
    score_scale = HD ** (-0.5)
    gain_first = attn_gain.astype(jnp.float32)
    gain_second = mlp_gain.astype(jnp.float32)
    input_full = block_in.astype(jnp.float32)
    input_share = lax.dynamic_slice_in_dim(input_full, share_start, share_len, 1)
    normed = rms_apply(input_full, gain_first).astype(jnp.bfloat16).reshape(row_count, model_width)
    query_raw = jnp.dot(normed, query_weight, preferred_element_type=jnp.float32).reshape(
        seq_count, ctx_tok, query_heads, HD
    )
    key_raw = jnp.dot(normed, key_weight, preferred_element_type=jnp.float32).reshape(
        seq_count, ctx_tok, key_heads, HD
    )
    value_raw = jnp.dot(normed, value_weight, preferred_element_type=jnp.float32)
    positions = lax.axis_index("ctx") * ctx_tok + jnp.arange(ctx_tok, dtype=jnp.int32)
    cosine, sine_table = rope_tables(positions, HD)
    queries = (
        rotate(query_raw, cosine, sine_table)
        .astype(jnp.bfloat16)
        .reshape(seq_count, ctx_tok, key_heads, group_size, HD)
    )
    keys_local = (
        rotate(key_raw, cosine, sine_table)
        .astype(jnp.bfloat16)
        .reshape(seq_count, ctx_tok, key_heads * HD)
    )
    values_local = value_raw.astype(jnp.bfloat16).reshape(seq_count, ctx_tok, key_heads * HD)
    keys_all, values_all = (
        lax.all_gather(keys_local, "ctx", axis=1, tiled=True),
        lax.all_gather(values_local, "ctx", axis=1, tiled=True),
    )
    seq_len = keys_all.shape[1]
    keys_all = keys_all.reshape(seq_count, seq_len, key_heads, HD)
    values_all = values_all.reshape(seq_count, seq_len, key_heads, HD)
    causal = positions[:, None] >= jnp.arange(seq_len, dtype=jnp.int32)[None, :]

    def scored(query_seq, key_seq):
        raw_scores = (
            jnp.einsum("qkgd,skd->kgqs", query_seq, key_seq, preferred_element_type=jnp.float32)
            * score_scale
        )
        return jnp.where(causal, raw_scores, -1e30)

    def forward_one(seq_parts):
        query_seq, key_seq, value_seq = seq_parts
        masked = scored(query_seq, key_seq)
        row_max = jnp.max(masked, axis=-1, keepdims=True)
        unnormed = jnp.exp(masked - row_max)
        row_total = jnp.sum(unnormed, axis=-1, keepdims=True)
        probs_low = (unnormed / row_total).astype(jnp.bfloat16)
        attended_seq = jnp.einsum(
            "kgqs,skd->qkgd", probs_low, value_seq, preferred_element_type=jnp.float32
        )
        return (attended_seq.astype(jnp.bfloat16), row_max, row_total)

    attended, row_maxes, row_totals = lax.map(forward_one, (queries, keys_all, values_all))
    attended_flat = attended.reshape(row_count, query_heads * HD)
    branch_part = jnp.dot(attended_flat, output_weight, preferred_element_type=jnp.float32).reshape(
        seq_count, ctx_tok, model_width
    )
    branch_full = lax.psum(branch_part, "tensor")
    hidden_full = input_full + branch_full
    normed_mlp = (
        rms_apply(hidden_full, gain_second).astype(jnp.bfloat16).reshape(row_count, model_width)
    )
    hidden_share = lax.dynamic_slice_in_dim(hidden_full, share_start, share_len, 1)
    gate_val = jnp.dot(normed_mlp, gate_weight, preferred_element_type=jnp.float32)
    up_val = jnp.dot(normed_mlp, up_weight, preferred_element_type=jnp.float32)
    activated = gated(gate_val, up_val).astype(jnp.bfloat16)
    mlp_part = jnp.dot(activated, down_weight, preferred_element_type=jnp.float32).reshape(
        seq_count, ctx_tok, model_width
    )
    mlp_full = lax.psum(mlp_part.astype(jnp.bfloat16), "tensor").astype(jnp.float32)
    mlp_share = lax.dynamic_slice_in_dim(mlp_full, share_start, share_len, 1)
    block_out = (hidden_share + mlp_share).astype(jnp.bfloat16)
    cotangent_rows = cotangent.reshape(row_count, model_width)
    cotangent_share = lax.dynamic_slice_in_dim(cotangent, share_start, share_len, 1).astype(
        jnp.float32
    )
    grad_down = rows_product(activated, cotangent_rows)
    grad_activated = back_product(cotangent_rows, down_weight)
    grad_gate_val, grad_up_val = jax.vjp(gated, gate_val, up_val)[1](grad_activated)
    grad_gate_val = grad_gate_val.astype(jnp.bfloat16)
    grad_up_val = grad_up_val.astype(jnp.bfloat16)
    grad_gate = rows_product(normed_mlp, grad_gate_val)
    grad_up = rows_product(normed_mlp, grad_up_val)
    grad_normed_mlp = (
        back_product(grad_gate_val, gate_weight) + back_product(grad_up_val, up_weight)
    ).reshape(seq_count, ctx_tok, model_width)
    grad_normed_share = lax.psum_scatter(
        grad_normed_mlp.astype(jnp.bfloat16), "tensor", scatter_dimension=1, tiled=True
    ).astype(jnp.float32)
    grad_hidden_norm, mlp_gain_part = jax.vjp(rms_apply, hidden_share, gain_second)[1](
        grad_normed_share
    )
    grad_hidden = cotangent_share + grad_hidden_norm
    grad_branch = lax.all_gather(
        grad_hidden.astype(jnp.bfloat16), "tensor", axis=1, tiled=True
    ).reshape(row_count, model_width)
    grad_output = rows_product(attended_flat, grad_branch)
    grad_attended = (
        back_product(grad_branch, output_weight)
        .astype(jnp.bfloat16)
        .reshape(seq_count, ctx_tok, key_heads, group_size, HD)
    )

    def backward_one(seq_parts):
        query_seq, key_seq, value_seq, grad_seq, row_max, row_total = seq_parts
        masked = scored(query_seq, key_seq)
        attn_probs = jnp.exp(masked - row_max) / row_total
        probs_low = attn_probs.astype(jnp.bfloat16)
        grad_probs = jnp.einsum(
            "qkgd,skd->kgqs", grad_seq, value_seq, preferred_element_type=jnp.float32
        )
        inner_sum = jnp.sum(attn_probs * grad_probs, axis=-1, keepdims=True)
        grad_scores = (attn_probs * (grad_probs - inner_sum)).astype(jnp.bfloat16)
        grad_query_seq = (
            jnp.einsum("kgqs,skd->qkgd", grad_scores, key_seq, preferred_element_type=jnp.float32)
            * score_scale
        )
        grad_key_seq = (
            jnp.einsum("kgqs,qkgd->skd", grad_scores, query_seq, preferred_element_type=jnp.float32)
            * score_scale
        )
        grad_value_seq = jnp.einsum(
            "kgqs,qkgd->skd", probs_low, grad_seq, preferred_element_type=jnp.float32
        )
        return (grad_query_seq, grad_key_seq, grad_value_seq)

    grad_queries, grad_keys, grad_values = lax.map(
        backward_one, (queries, keys_all, values_all, grad_attended, row_maxes, row_totals)
    )
    key_grads, value_grads = (
        lax.psum_scatter(
            grad_keys.reshape(seq_count, seq_len, key_heads * HD).astype(jnp.bfloat16),
            "ctx",
            scatter_dimension=1,
            tiled=True,
        ).astype(jnp.float32),
        lax.psum_scatter(
            grad_values.reshape(seq_count, seq_len, key_heads * HD).astype(jnp.bfloat16),
            "ctx",
            scatter_dimension=1,
            tiled=True,
        ).astype(jnp.float32),
    )
    grad_query_raw = (
        unrotate(grad_queries.reshape(seq_count, ctx_tok, query_heads, HD), cosine, sine_table)
        .astype(jnp.bfloat16)
        .reshape(row_count, query_heads * HD)
    )
    grad_key_raw = (
        unrotate(key_grads.reshape(seq_count, ctx_tok, key_heads, HD), cosine, sine_table)
        .astype(jnp.bfloat16)
        .reshape(row_count, key_heads * HD)
    )
    grad_value_raw = value_grads.astype(jnp.bfloat16).reshape(row_count, key_heads * HD)
    grad_query = rows_product(normed, grad_query_raw)
    grad_key = rows_product(normed, grad_key_raw)
    grad_value = rows_product(normed, grad_value_raw)
    grad_normed = (
        back_product(grad_query_raw, query_weight)
        + back_product(grad_key_raw, key_weight)
        + back_product(grad_value_raw, value_weight)
    )
    grad_normed_attn = lax.psum_scatter(
        grad_normed.reshape(seq_count, ctx_tok, model_width).astype(jnp.bfloat16),
        "tensor",
        scatter_dimension=1,
        tiled=True,
    ).astype(jnp.float32)
    grad_input_norm, attn_gain_part = jax.vjp(rms_apply, input_share, gain_first)[1](
        grad_normed_attn
    )
    input_grad = grad_hidden + grad_input_norm
    attn_gain_sum, mlp_gain_sum = lax.psum((attn_gain_part, mlp_gain_part), "tensor")
    grad_attn_gain, grad_query, grad_key, grad_value, grad_output = (
        lax.psum_scatter(
            attn_gain_sum.astype(jnp.bfloat16), ("dp", "ctx"), scatter_dimension=0, tiled=True
        ).astype(jnp.float32),
        lax.psum_scatter(
            grad_query.astype(jnp.bfloat16), ("dp", "ctx"), scatter_dimension=0, tiled=True
        ).astype(jnp.float32),
        lax.psum_scatter(
            grad_key.astype(jnp.bfloat16), ("dp", "ctx"), scatter_dimension=0, tiled=True
        ).astype(jnp.float32),
        lax.psum_scatter(
            grad_value.astype(jnp.bfloat16), ("dp", "ctx"), scatter_dimension=0, tiled=True
        ).astype(jnp.float32),
        lax.psum_scatter(
            grad_output.astype(jnp.bfloat16), ("dp", "ctx"), scatter_dimension=1, tiled=True
        ).astype(jnp.float32),
    )
    grad_mlp_gain, grad_gate, grad_up, grad_down = (
        lax.psum_scatter(
            mlp_gain_sum.astype(jnp.bfloat16), ("dp", "ctx"), scatter_dimension=0, tiled=True
        ).astype(jnp.float32),
        lax.psum_scatter(
            grad_gate.astype(jnp.bfloat16), ("dp", "ctx"), scatter_dimension=0, tiled=True
        ).astype(jnp.float32),
        lax.psum_scatter(
            grad_up.astype(jnp.bfloat16), ("dp", "ctx"), scatter_dimension=0, tiled=True
        ).astype(jnp.float32),
        lax.psum_scatter(
            grad_down.astype(jnp.bfloat16), ("dp", "ctx"), scatter_dimension=1, tiled=True
        ).astype(jnp.float32),
    )
    return (
        block_out,
        input_grad,
        grad_attn_gain,
        grad_query,
        grad_key,
        grad_value,
        grad_output,
        grad_mlp_gain,
        grad_gate,
        grad_up,
        grad_down,
    )


def solution(mesh):
    in_specs = (
        P("dp", "ctx", None),
        P(),
        P(None, "tensor"),
        P(None, "tensor"),
        P(None, "tensor"),
        P("tensor", None),
        P(),
        P(None, "tensor"),
        P(None, "tensor"),
        P("tensor", None),
        P("dp", "ctx", None),
    )
    out_specs = (
        P("dp", ("ctx", "tensor"), None),
        P("dp", ("ctx", "tensor"), None),
        P(("dp", "ctx")),
        P(("dp", "ctx"), "tensor"),
        P(("dp", "ctx"), "tensor"),
        P(("dp", "ctx"), "tensor"),
        P("tensor", ("dp", "ctx")),
        P(("dp", "ctx")),
        P(("dp", "ctx"), "tensor"),
        P(("dp", "ctx"), "tensor"),
        P("tensor", ("dp", "ctx")),
    )
    return jax.shard_map(shards, mesh=mesh, in_specs=in_specs, out_specs=out_specs, check_vma=False)
```

profile of v0, /device:TPU:0, one launch (start us, length us, event | category | flops | bytes accessed | tf_op | source)
XLA Modules:
  0.0 1205.2 jit_solution(18052716655228510555)
XLA Ops:
  11.7 18.0 %all_gather.9 = bf16[2,512,256]{2,1,0:T(8,128)(2,1)} all-gather(bf16[2,128,256]{2,1,0:T(8,128)(2,1)S(1)} %bitcast.319), channel_id=1, replica_groups=mesh['dp'=4,'ctx'=4,'tensor'=2] {'ctx'}, dimensions={1}, use_global_device_ids=true | all-gather | bytes 655360 | tf_op jit(solution)/shard_map/all_gather | solution.py:115
  29.7 2.1 copy.52
  35.1 15.3 %all_gather.10 = bf16[2,512,256]{1,2,0:T(8,128)(2,1)S(1)} all-gather(bf16[2,128,256]{1,2,0:T(8,128)(2,1)S(1)} %bitcast.320), channel_id=1, replica_groups=mesh['dp'=4,'ctx'=4,'tensor'=2] {'ctx'}, dimensions={1}, use_global_device_ids=true | all-gather | bytes 655360 | tf_op jit(solution)/shard_map/all_gather | solution.py:114
  50.4 6.5 copy.54
  56.9 3.5 fusion.79
  60.6 7.6 while.30
  68.2 5.3 fusion.63
  73.9 63.4 %all-reduce.7.cloned.1.call-done = f32[2,128,2048]{2,1,0:T(8,128)} async-done(((f32[2,128,2048]{2,1,0:T(8,128)}), f32[2,128,2048]{2,1,0:T(8,128)}) %all-reduce.7.cloned.1.call-update) | async-done | bytes 2097168 | tf_op jit(solution)/shard_map/psum | solution.py:146
  137.2 2.2 multiply_reduce_fusion
  139.8 10.8 fusion.99
  152.0 6.1 fusion.98
  158.1 13.5 %multiply_convert_fusion = (bf16[256,4096]{1,0:T(8,128)(2,1)}, bf16[256,4096]{1,0:T(8,128)(2,1)}, bf16[256,4096]{1,0:T(8,128)(2,1)}) fusion(f32[256,4096]{1,0:T(8,128)} %fusion.98, f32[256,4096]{1,0:T(8,128)} %fusion.99, bf16[256,2048]{1,0:T(8,128)(2,1)S(1)} %bitcast.299, bf16[4096,2048]{1,0:T(8,128)(2,1)} %param.24), kind=kOutput, calls=%fused_computation.77 | convolution fusion | flops 4311744512 | bytes 32505856 | tf_op jit(solution)/shard_map/dot_general | solution.py:61
  171.6 12.3 %fusion.100 = f32[256,2048]{1,0:T(8,128)} fusion(bf16[256,4096]{1,0:T(8,128)(2,1)} %get-tuple-element.254, bf16[2048,4096]{1,0:T(8,128)(2,1)} %param.22), kind=kOutput, calls=%fused_computation.163 | convolution fusion | flops 4294967296 | bytes 20971520 | tf_op jit(solution)/shard_map/dot_general | solution.py:61
  183.9 12.4 %fusion.66 = bf16[256,2048]{1,0:T(8,128)(2,1)} fusion(f32[256,2048]{1,0:T(8,128)} %fusion.100, bf16[256,4096]{1,0:T(8,128)(2,1)} %get-tuple-element.253, bf16[2048,4096]{1,0:T(8,128)(2,1)} %param.23), kind=kOutput, calls=%fused_computation.87 | convolution fusion | flops 4296015872 | bytes 22020096 | tf_op jit(solution)/shard_map/dot_general | solution.py:61
  196.6 20.3 %reduce-scatter.18.cloned.1.call-done = bf16[2,64,2048]{2,1,0:T(8,128)(2,1)} async-done(((bf16[2,128,2048]{2,1,0:T(8,128)(2,1)}), bf16[2,64,2048]{2,1,0:T(8,128)(2,1)}) %reduce-scatter.18.cloned.1.call-update) | async-done | bytes 524304 | tf_op jit(solution)/shard_map/reduce_scatter | solution.py:175
  218.3 2.4 fusion.94
  220.8 21.4 %all-gather.2.cloned.1.call-done = bf16[2,128,2048]{2,1,0:T(8,128)(2,1)} async-done(((bf16[2,64,2048]{2,1,0:T(8,128)(2,1)}), bf16[2,128,2048]{2,1,0:T(8,128)(2,1)}) %all-gather.2.cloned.1.call-update) | async-done | bytes 1048592 | tf_op jit(solution)/shard_map/all_gather | solution.py:182
  242.1 4.6 convolution_convert_fusion.7
  246.7 3.4 reshape.265
  250.1 2.6 copy.57
  252.7 16.5 %while.31 = (s32[]{:T(128)}, f32[2,128,4,4,64]{1,4,3,2,0:T(8,128)}, bf16[2,512,4,64]{1,3,2,0:T(8,128)(2,1)}, bf16[2,512,4,64]{1,3,2,0:T(8,128)(2,1)}, bf16[2,512...) while((s32[]{:T(128)}, f32[2,128,4,4,64]{1,4,3,2,0:T(8,128)}, ...), condition=%wide.region_13.14_spmd.clone, body=%wide.region_11.13_spmd.clone.sunk | while | flops 681900032 | bytes 58136444 | solution.py:215
  273.2 2.0 copy.60
  275.3 19.8 %reduce-scatter.34.cloned.1.call-done = bf16[128,512]{1,0:T(8,128)(2,1)} async-done(((bf16[512,512]{1,0:T(8,128)(2,1)}), bf16[128,512]{1,0:T(8,128)(2,1)}) %reduce-scatter.34.cloned.1.call-update) | async-done | bytes 131088
  296.5 2.7 convolution_convert_fusion.6
  299.2 18.2 %reduce-scatter.20.cloned.1.call-done = bf16[2,128,256]{2,1,0:T(8,128)(2,1)} async-done(((bf16[2,512,256]{2,1,0:T(8,128)(2,1)}), bf16[2,128,256]{2,1,0:T(8,128)(2,1)}) %reduce-scatter.20.cloned.1.call-update) | async-done | bytes 131088 | tf_op jit(solution)/shard_map/reduce_scatter | solution.py:225
  317.4 2.7 fusion.68
  322.2 3.7 fusion.86
  328.5 12.2 %convolution_convert_fusion.5 = bf16[256,2048]{1,0:T(8,128)(2,1)} fusion(bf16[256,4096]{1,0:T(8,128)(2,1)} %get-tuple-element.255, bf16[4096,2048]{1,0:T(8,128)(2,1)} %param.24), kind=kOutput, calls=%fused_computation.88 | convolution fusion | flops 4295491584 | bytes 19922944 | tf_op jit(solution)/shard_map/dot_general | solution.py:155
  342.4 4.4 convolution_convert_fusion.3
  346.8 6.4 copy.80
  353.3 4.7 convolution_convert_fusion.4
  358.1 12.2 %convolution_convert_fusion = bf16[4096,2048]{1,0:T(8,128)(2,1)} fusion(bf16[256,4096]{1,0:T(8,128)(2,1)} %get-tuple-element.255, bf16[256,2048]{1,0:T(8,128)(2,1)} %bitcast.298), kind=kOutput, calls=%fused_computation.68 | convolution fusion | flops 4303355904 | bytes 19922944 | tf_op jit(solution)/shard_map/dot_general | solution.py:55
  370.2 20.9 %copy.82 = bf16[4096,2048]{0,1:T(8,128)(2,1)} copy(bf16[4096,2048]{1,0:T(8,128)(2,1)} %convolution_convert_fusion) | data formatting | bytes 33554432
  391.5 12.3 %convolution_convert_fusion.1 = bf16[2048,4096]{1,0:T(8,128)(2,1)} fusion(bf16[256,2048]{1,0:T(8,128)(2,1)} %bitcast.294, bf16[256,4096]{1,0:T(8,128)(2,1)} %get-tuple-element.253), kind=kOutput, calls=%fused_computation.69 | convolution fusion | flops 4303355904 | bytes 19922944 | tf_op jit(solution)/shard_map/dot_general | solution.py:55
  403.8 12.2 %convolution_convert_fusion.2 = bf16[2048,4096]{1,0:T(8,128)(2,1)} fusion(bf16[256,2048]{1,0:T(8,128)(2,1)} %bitcast.295, bf16[256,4096]{1,0:T(8,128)(2,1)} %get-tuple-element.254), kind=kOutput, calls=%fused_computation.70 | convolution fusion | flops 4303355904 | bytes 19922944 | tf_op jit(solution)/shard_map/dot_general | solution.py:55
  416.1 2.8 convert_element_type.192
  423.0 14.0 %reduce-scatter.28.cloned.1.call-done = bf16[128,256]{1,0:T(8,128)(2,1)} async-done(((bf16[2048,256]{1,0:T(8,128)(2,1)}), bf16[128,256]{1,0:T(8,128)(2,1)}) %reduce-scatter.28.cloned.1.call-update) | async-done | bytes 65552 | tf_op jit(solution)/shard_map/reduce_scatter | solution.py:272
  438.5 20.8 %reduce-scatter.22.cloned.1.call-done = bf16[2,64,2048]{2,1,0:T(8,128)(2,1)} async-done(((bf16[2,128,2048]{2,1,0:T(8,128)(2,1)}), bf16[2,64,2048]{2,1,0:T(8,128)(2,1)}) %reduce-scatter.22.cloned.1.call-update) | async-done | bytes 524304 | tf_op jit(solution)/shard_map/reduce_scatter | solution.py:251
  461.0 6.9 all-reduce.2
  468.0 32.6 %all-reduce.3 = (bf16[2048]{0:T(1024)(128)(2,1)S(1)}, bf16[2048]{0:T(1024)(128)(2,1)S(1)}) all-reduce(bf16[2048]{0:T(1024)(128)(2,1)S(1)} %get-tuple-element.239, bf16[2048]{0:T(1024)(128)(2,1)S(1)} %get-tuple-element.240), channel_id=6, replica_groups=mesh['dp'=4,'ctx'=4,'tensor'=2] {'dp','ctx'}, use_global_device_ids=true, to_apply=%region_21.22.clone | all-reduce | flops 4096 | bytes 16384
  501.8 3.5 fusion.78
  505.3 73.1 %reduce-scatter.36.cloned.1.call-done = bf16[128,1024]{1,0:T(8,128)(2,1)} async-done(((bf16[2048,1024]{1,0:T(8,128)(2,1)}), bf16[128,1024]{1,0:T(8,128)(2,1)}) %reduce-scatter.36.cloned.1.call-update) | async-done | bytes 262160
  580.3 73.8 %reduce-scatter.24.cloned.1.call-done = bf16[128,1024]{1,0:T(8,128)(2,1)} async-done(((bf16[2048,1024]{1,0:T(8,128)(2,1)}), bf16[128,1024]{1,0:T(8,128)(2,1)}) %reduce-scatter.24.cloned.1.call-update) | async-done | bytes 262160 | tf_op jit(solution)/shard_map/reduce_scatter | solution.py:266
  655.9 178.6 %reduce-scatter.38.cloned.1.call-done = bf16[128,4096]{1,0:T(8,128)(2,1)} async-done(((bf16[2048,4096]{1,0:T(8,128)(2,1)}), bf16[128,4096]{1,0:T(8,128)(2,1)}) %reduce-scatter.38.cloned.1.call-update) | async-done | bytes 1048592
  837.5 177.5 %reduce-scatter.32.cloned.1.call-done = bf16[128,4096]{1,0:T(8,128)(2,1)} async-done(((bf16[2048,4096]{1,0:T(8,128)(2,1)}), bf16[128,4096]{1,0:T(8,128)(2,1)}) %reduce-scatter.32.cloned.1.call-update) | async-done | bytes 1048592 | tf_op jit(solution)/shard_map/reduce_scatter | solution.py:286
  1015.0 2.8 convert_element_type.239
  1017.8 177.7 %reduce-scatter.30.cloned.1.call-done = bf16[128,4096]{1,0:T(8,128)(2,1)} async-done(((bf16[2048,4096]{1,0:T(8,128)(2,1)}), bf16[128,4096]{1,0:T(8,128)(2,1)}) %reduce-scatter.30.cloned.1.call-update) | async-done | bytes 1048592 | tf_op jit(solution)/shard_map/reduce_scatter | solution.py:283
  1195.5 2.8 convert_element_type.237
  (204 shorter events, 62.2 us)
Async XLA Ops:
  7.2 4.1 copy-start
  7.2 24.6 %copy-start.10 = (bf16[2048,256]{1,0:T(8,128)(2,1)S(1)}, bf16[2048,256]{1,0:T(8,128)(2,1)}, u32[]{:S(2)}) copy-start(bf16[2048,256]{1,0:T(8,128)(2,1)} %param.18) | copy-start | bytes 3145732
  7.2 130.0 %all-reduce.7.cloned.1.call-start = ((), (), s32[]{:S(2)}) async-start(), calls=%async_computation.11 | async-start | bytes 4194304 | tf_op jit(solution)/shard_map/psum | solution.py:146
  9.7 1.5 copy-start.26
  11.2 45.7 %copy-start.1 = (bf16[2,128,2048]{2,1,0:T(8,128)(2,1)}, bf16[2,128,2048]{2,1,0:T(8,128)(2,1)S(1)}, u32[]{:S(2)}) copy-start(bf16[2,128,2048]{2,1,0:T(8,128)(2,1)S(1)} %multiply_convert_fusion.3) | copy-start | bytes 3145732
  35.0 25.4 %copy-start.22 = (f32[128,32]{0,1:T(8,128)}, f32[128,32]{0,1:T(8,128)S(1)}, u32[]{:S(2)}) copy-start(f32[128,32]{0,1:T(8,128)S(1)} %get-tuple-element.266) | copy-start | bytes 49156
  35.0 25.4 %copy-start.24 = (f32[128,32]{0,1:T(8,128)}, f32[128,32]{0,1:T(8,128)S(1)}, u32[]{:S(2)}) copy-start(f32[128,32]{0,1:T(8,128)S(1)} %get-tuple-element.267) | copy-start | bytes 49156
  60.7 1.7 copy-start.8
  60.7 1.7 copy-start.13
  64.5 1.7 copy-start.8
  64.5 1.7 copy-start.13
  68.2 5.4 copy-start.3
  68.2 5.4 copy-start.5
  68.2 5.6 copy-start.28
  73.6 143.3 %reduce-scatter.18.cloned.1.call-start = ((), (), s32[]{:S(2)}) async-start(), calls=%async_computation.13 | async-start | bytes 1572864 | tf_op jit(solution)/shard_map/reduce_scatter | solution.py:175
  139.5 11.1 slice-start
  139.7 10.9 copy-start.7
  139.7 10.9 slice-start.1
  139.8 10.9 slice-start.2
  139.8 12.2 %slice-start.3 = ((s8[16777216]{0:T(1024)(128)(4,1)}), s8[4194304]{0:T(1024)(128)(4,1)S(1)}, s32[]{:S(2)}) async-start(s8[16777216]{0:T(1024)(128)(4,1)} %bitcast.326), calls=%async_computation.28 | async-start | bytes 8388608
  152.0 6.1 copy-start.9
  196.4 45.8 %all-gather.2.cloned.1.call-start = ((), (), s32[]{:S(2)}) async-start(), calls=%async_computation.14 | async-start | bytes 1572864 | tf_op jit(solution)/shard_map/all_gather | solution.py:182
  220.7 74.5 %reduce-scatter.34.cloned.1.call-start = ((), (), s32[]{:S(2)}) async-start(), calls=%async_computation.22 | async-start | bytes 655360
  252.7 1.9 copy-start.4
  252.7 1.9 copy-start.6
  256.2 1.2 copy-start.18
  257.4 1.8 copy-start.15
  258.4 1.3 copy-start.19
  261.0 1.9 copy-start.4
  261.0 1.9 copy-start.6
  265.6 1.8 copy-start.15
  266.7 1.2 copy-start.19
  269.2 27.1 %copy-start.23 = (f32[128,32]{0,1:T(8,128)S(1)}, f32[128,32]{0,1:T(8,128)}, u32[]{:S(2)}) copy-start(f32[128,32]{0,1:T(8,128)} %copy-done.22) | copy-start | bytes 49156
  269.2 27.1 %copy-start.25 = (f32[128,32]{0,1:T(8,128)S(1)}, f32[128,32]{0,1:T(8,128)}, u32[]{:S(2)}) copy-start(f32[128,32]{0,1:T(8,128)} %copy-done.24) | copy-start | bytes 49156
  273.2 44.3 %reduce-scatter.20.cloned.1.call-start = ((), (), s32[]{:S(2)}) async-start(), calls=%async_computation.15 | async-start | bytes 655360 | tf_op jit(solution)/shard_map/reduce_scatter | solution.py:225
  275.3 146.2 %reduce-scatter.26.cloned.1.call-start = ((), (), s32[]{:S(2)}) async-start(), calls=%async_computation.18 | async-start | bytes 1114112 | tf_op jit(solution)/shard_map/reduce_scatter | solution.py:269
  299.2 137.8 %reduce-scatter.28.cloned.1.call-start = ((), (), s32[]{:S(2)}) async-start(), calls=%async_computation.19 | async-start | bytes 1114112 | tf_op jit(solution)/shard_map/reduce_scatter | solution.py:272
  320.2 139.1 %reduce-scatter.22.cloned.1.call-start = ((), (), s32[]{:S(2)}) async-start(), calls=%async_computation.16 | async-start | bytes 1572864 | tf_op jit(solution)/shard_map/reduce_scatter | solution.py:251
  321.6 4.3 copy-start.11
  322.2 4.2 copy-start.12
  328.3 173.5 %all-reduce.9.cloned.1.call-start = ((), (), s32[]{:S(2)}) async-start(), calls=%async_computation.12 | async-start | bytes 2097152 | tf_op jit(solution)/shard_map/psum | solution.py:158
  340.8 237.6 %reduce-scatter.36.cloned.1.call-start = ((), (), s32[]{:S(2)}) async-start(), calls=%async_computation.23 | async-start | bytes 4456448
  353.3 300.8 %reduce-scatter.24.cloned.1.call-start = ((), (), s32[]{:S(2)}) async-start(), calls=%async_computation.17 | async-start | bytes 4456448 | tf_op jit(solution)/shard_map/reduce_scatter | solution.py:266
  358.0 476.4 %reduce-scatter.38.cloned.1.call-start = ((), (), s32[]{:S(2)}) async-start(), calls=%async_computation.24 | async-start | bytes 17825792
  391.2 623.9 %reduce-scatter.32.cloned.1.call-start = ((), (), s32[]{:S(2)}) async-start(), calls=%async_computation.21 | async-start | bytes 17825792 | tf_op jit(solution)/shard_map/reduce_scatter | solution.py:286
  403.8 791.7 %reduce-scatter.30.cloned.1.call-start = ((), (), s32[]{:S(2)}) async-start(), calls=%async_computation.20 | async-start | bytes 17825792 | tf_op jit(solution)/shard_map/reduce_scatter | solution.py:283
  416.0 2.9 copy-start.29
  416.0 43.3 %copy-start.27 = (f32[2048]{0:T(1024)S(1)}, f32[2048]{0:T(1024)}, u32[]{:S(2)}) copy-start(f32[2048]{0:T(1024)} %copy-done.26) | copy-start | bytes 24580
  (12 other events, 11.4 us)
Sparse Core Ops, SparseCore 0:
  73.7 63.5 all-reduce.6
  196.5 20.3 reduce-scatter.17
  220.8 21.2 all-gather.1
  273.3 21.8 reduce-scatter.33
  297.3 20.1 reduce-scatter.19
  320.9 55.7 reduce-scatter.25
  380.4 56.6 reduce-scatter.27
  439.8 19.4 reduce-scatter.21
  461.6 40.1 all-reduce.8
  505.5 72.7 reduce-scatter.35
  582.2 71.8 reduce-scatter.23
  658.1 176.3 reduce-scatter.37
  838.6 176.4 reduce-scatter.31
  1019.0 176.4 reduce-scatter.29
where the time goes:
time: 1210 us
  waiting for transfers between devices  859 us (71%)
  matrix products  154 us (13%)
  blocking collectives  72.8 us (6%)
  local copies, waits for them, and re-layouts  63.8 us (5%)
  other arithmetic  37.8 us (3%)
  between operations  15.6 us (1%)
    unnamed x17, waiting for transfers between devices  272 us
    reduce_scatter x1, waiting for transfers between devices, shards(): lax.psum_scatter(grad_gate.astype(jnp.bfloat16), ('dp', 'ctx'), scatter_d...  178 us
    reduce_scatter x1, waiting for transfers between devices, shards(): lax.psum_scatter(grad_up.astype(jnp.bfloat16), ('dp', 'ctx'), scatter_dim...  178 us
    reduce_scatter x1, waiting for transfers between devices, shards(): lax.psum_scatter(grad_query.astype(jnp.bfloat16), ('dp', 'ctx'), scatter_...  73.8 us
    psum x1, waiting for transfers between devices, shards(): branch_full = lax.psum(branch_part, 'tensor')  63.4 us
    dot_general x7, matrix products, rows_product(): lax.dot_general(left, right, (((0,), (0,)), ((), ())), preferred_element_...  51.1 us
    dot_general x7, matrix products, back_product(): lax.dot_general(left, right, (((1,), (1,)), ((), ())), preferred_element_...  48.4 us
    unnamed x56, local copies, waits for them, and re-layouts  48 us
  transfers between devices with their start and end apart: 14, of which 13 were waited for; matrix products, arithmetic and copies ran while one was open for 10% of the time, Pallas kernels for 0%

commit v1 on v0

v1 whole, which is shorter than its diff:
```python
import jax
import jax.numpy as jnp
from jax import lax
from jax.sharding import PartitionSpec as P

HD = 64

norm_eps = 1e-05
rope_base = 500000.0
f32 = jnp.float32
bf16 = jnp.bfloat16


def rms_apply(values, gain):
    return values * lax.rsqrt(jnp.mean(values * values, axis=-1, keepdims=True) + norm_eps) * gain


def rope_tables(positions, head_size):
    half_width = head_size // 2
    frequency = rope_base ** (-jnp.arange(half_width, dtype=f32) * 2.0 / head_size)
    angles = positions.astype(f32)[:, None] * frequency[None, :]
    return (jnp.cos(angles)[:, None, :], jnp.sin(angles)[:, None, :])


def rotate(vectors, cosine, sine_table):
    half_width = vectors.shape[-1] // 2
    first_half = vectors[..., :half_width]
    second_half = vectors[..., half_width:]
    return jnp.concatenate(
        [
            first_half * cosine - second_half * sine_table,
            second_half * cosine + first_half * sine_table,
        ],
        axis=-1,
    )


def dot_nn(left, right):
    return lax.dot_general(left, right, (((1,), (0,)), ((), ())), preferred_element_type=f32)


def dot_tn(left, right):
    return lax.dot_general(left, right, (((0,), (0,)), ((), ())), preferred_element_type=f32)


def dot_nt(left, right):
    return lax.dot_general(left, right, (((1,), (1,)), ((), ())), preferred_element_type=f32)


def xor_pairs(count, bit):
    return [(i, i ^ bit) for i in range(count)]


def dp_bits():
    count = lax.axis_size("dp")
    bits = []
    bit = count // 2
    while bit:
        bits.append(bit)
        bit //= 2
    return count, bits


def dp_rows(rows):
    count, bits = dp_bits()
    for bit in bits:
        rows = jnp.concatenate([rows, lax.ppermute(rows, "dp", xor_pairs(count, bit))], axis=0)
    return rows


def dp_columns(rows):
    count, bits = dp_bits()
    me = lax.axis_index("dp")
    for bit in bits:
        half = rows.shape[1] // 2
        upper = (me // bit) % 2
        keep = lax.dynamic_slice_in_dim(rows, upper * half, half, 1)
        give = lax.dynamic_slice_in_dim(rows, (1 - upper) * half, half, 1)
        rows = jnp.concatenate([keep, lax.ppermute(give, "dp", xor_pairs(count, bit))], axis=0)
    return rows


def swap_tensor(values):
    return lax.ppermute(values, "tensor", [(0, 1), (1, 0)])


def sum_share(part):
    ranks = lax.axis_size("tensor")
    if ranks != 2:
        return lax.psum_scatter(part.astype(bf16), "tensor", scatter_dimension=1, tiled=True).astype(f32)
    share = part.shape[1] // 2
    me = lax.axis_index("tensor")
    mine = lax.dynamic_slice_in_dim(part, me * share, share, 1)
    theirs = lax.dynamic_slice_in_dim(part, (1 - me) * share, share, 1)
    return mine + swap_tensor(theirs.astype(bf16)).astype(f32)


def sum_whole(part):
    if lax.axis_size("tensor") != 2:
        return lax.psum(part.astype(bf16), "tensor").astype(f32)
    low = part.astype(bf16)
    return low.astype(f32) + swap_tensor(low).astype(f32)


def other_weight(weight):
    count, _ = dp_bits()
    half = weight.shape[0] // 2
    parity = lax.axis_index("dp") % 2
    got = swap_tensor(lax.dynamic_slice_in_dim(weight, parity * half, half, 0))
    also = lax.ppermute(got, "dp", xor_pairs(count, 1))
    even = parity == 0
    return jnp.concatenate([jnp.where(even, got, also), jnp.where(even, also, got)], axis=0)


def ctx_scatter(block):
    return lax.psum_scatter(block.astype(bf16), "ctx", scatter_dimension=0, tiled=True).astype(f32)


def shards(
    block_in,
    attn_gain,
    query_weight,
    key_weight,
    value_weight,
    output_weight,
    mlp_gain,
    gate_weight,
    up_weight,
    down_weight,
    cotangent,
):
    seq_count, ctx_tok, width = block_in.shape
    ctx_ranks = lax.axis_size("ctx")
    tensor_ranks = lax.axis_size("tensor")
    share_len = ctx_tok // tensor_ranks
    share_start = lax.axis_index("tensor") * share_len
    rows = seq_count * ctx_tok
    query_heads = query_weight.shape[1] // HD
    key_heads = key_weight.shape[1] // HD
    kv_cols = key_heads * HD
    group = query_heads // key_heads
    scale = HD ** (-0.5)
    ctx_at = lax.axis_index("ctx")

    def share_of(values):
        return lax.dynamic_slice_in_dim(values, share_start, share_len, 1)

    gain_first = attn_gain.astype(f32)
    gain_second = mlp_gain.astype(f32)
    input_full = block_in.astype(f32)
    cot_rows = cotangent.reshape(rows, width)
    r_first = lax.rsqrt(jnp.mean(input_full * input_full, axis=-1, keepdims=True) + norm_eps)
    unit_first = input_full * r_first
    normed = (unit_first * gain_first).astype(bf16).reshape(rows, width)

    key_raw = dot_nn(normed, key_weight).reshape(seq_count, ctx_tok, key_heads, HD)
    value_raw = dot_nn(normed, value_weight)
    positions = ctx_at * ctx_tok + jnp.arange(ctx_tok, dtype=jnp.int32)
    cosine, sine = rope_tables(positions, HD)
    keys_local = rotate(key_raw, cosine, sine).astype(bf16).reshape(seq_count, ctx_tok, kv_cols)
    kv_local = jnp.concatenate(
        [keys_local, value_raw.astype(bf16).reshape(seq_count, ctx_tok, kv_cols)], axis=-1
    )
    blocks = [kv_local]
    for back in range(1, ctx_ranks):
        blocks.append(
            lax.ppermute(kv_local, "ctx", [(i, i + back) for i in range(ctx_ranks - back)])
        )
    kv_all = jnp.concatenate(blocks, axis=1)
    seq_len = kv_all.shape[1]
    keys_all = kv_all[..., :kv_cols].reshape(seq_count, seq_len, key_heads, HD)
    values_all = kv_all[..., kv_cols:].reshape(seq_count, seq_len, key_heads, HD)
    query_raw = dot_nn(normed, query_weight).reshape(seq_count, ctx_tok, query_heads, HD)
    queries = (
        rotate(query_raw, cosine, sine)
        .astype(bf16)
        .reshape(seq_count, ctx_tok, key_heads, group, HD)
    )
    key_at = jnp.arange(seq_len, dtype=jnp.int32)
    key_back = key_at // ctx_tok
    query_at = jnp.arange(ctx_tok, dtype=jnp.int32)
    causal = jnp.where(
        key_back[None, :] == 0,
        query_at[:, None] >= key_at[None, :],
        (key_back <= ctx_at)[None, :],
    )

    def scored(query_seq, key_seq):
        raw = jnp.einsum("qkgd,skd->kgqs", query_seq, key_seq, preferred_element_type=f32) * scale
        return jnp.where(causal, raw, -1e30)

    def forward_one(seq_parts):
        query_seq, key_seq, value_seq = seq_parts
        masked = scored(query_seq, key_seq)
        row_max = jnp.max(masked, axis=-1, keepdims=True)
        unnormed = jnp.exp(masked - row_max)
        row_total = jnp.sum(unnormed, axis=-1, keepdims=True)
        probs_low = (unnormed / row_total).astype(bf16)
        attended_seq = jnp.einsum("kgqs,skd->qkgd", probs_low, value_seq, preferred_element_type=f32)
        return (attended_seq.astype(bf16), row_max, row_total)

    attended, row_maxes, row_totals = lax.map(forward_one, (queries, keys_all, values_all))
    attended_flat = attended.reshape(rows, query_heads * HD)
    branch = dot_nn(attended_flat, output_weight)
    if tensor_ranks == 2:
        branch = branch + dot_nn(swap_tensor(attended_flat), other_weight(output_weight))
    else:
        branch = lax.psum(branch, "tensor")
    hidden = input_full + branch.reshape(seq_count, ctx_tok, width)
    r_second = lax.rsqrt(jnp.mean(hidden * hidden, axis=-1, keepdims=True) + norm_eps)
    unit_second = hidden * r_second
    normed_mlp = (unit_second * gain_second).astype(bf16).reshape(rows, width)

    grad_activated = dot_nt(cot_rows, down_weight)
    gate_val = dot_nn(normed_mlp, gate_weight)
    up_val = dot_nn(normed_mlp, up_weight)
    sig = jax.nn.sigmoid(gate_val)
    silu = gate_val * sig
    activated = (silu * up_val).astype(bf16)
    grad_gate_val = (grad_activated * up_val * sig * (1.0 + gate_val * (1.0 - sig))).astype(bf16)
    grad_up_val = (grad_activated * silu).astype(bf16)
    mlp_part = dot_nn(activated, down_weight).reshape(seq_count, ctx_tok, width)
    grad_normed_part = (
        dot_nt(grad_gate_val, gate_weight) + dot_nt(grad_up_val, up_weight)
    ).reshape(seq_count, ctx_tok, width)
    mlp_gain_part = jnp.sum(grad_normed_part * unit_second, axis=(0, 1))

    act_all = dp_rows(activated)
    cot_cols = dp_columns(cot_rows)
    grad_down = ctx_scatter(dot_tn(cot_cols, act_all)).T
    nm_cols = dp_columns(normed_mlp)
    grad_gate = ctx_scatter(dot_tn(nm_cols, dp_rows(grad_gate_val)))
    grad_up = ctx_scatter(dot_tn(nm_cols, dp_rows(grad_up_val)))

    block_out = (share_of(hidden) + sum_share(mlp_part)).astype(bf16)
    grad_normed = sum_whole(grad_normed_part)
    scaled = gain_second * grad_normed
    grad_hidden = cotangent.astype(f32) + r_second * (
        scaled - unit_second * jnp.mean(scaled * unit_second, axis=-1, keepdims=True)
    )
    grad_branch = grad_hidden.astype(bf16).reshape(rows, width)
    grad_attended = (
        dot_nt(grad_branch, output_weight)
        .astype(bf16)
        .reshape(seq_count, ctx_tok, key_heads, group, HD)
    )
    grad_output = ctx_scatter(dot_tn(dp_columns(grad_branch), dp_rows(attended_flat))).T

    def backward_one(seq_parts):
        query_seq, key_seq, value_seq, grad_seq, row_max, row_total = seq_parts
        masked = scored(query_seq, key_seq)
        attn_probs = jnp.exp(masked - row_max) / row_total
        probs_low = attn_probs.astype(bf16)
        grad_probs = jnp.einsum("qkgd,skd->kgqs", grad_seq, value_seq, preferred_element_type=f32)
        inner_sum = jnp.sum(attn_probs * grad_probs, axis=-1, keepdims=True)
        grad_scores = (attn_probs * (grad_probs - inner_sum)).astype(bf16)
        grad_query_seq = (
            jnp.einsum("kgqs,skd->qkgd", grad_scores, key_seq, preferred_element_type=f32) * scale
        )
        grad_key_seq = (
            jnp.einsum("kgqs,qkgd->skd", grad_scores, query_seq, preferred_element_type=f32) * scale
        )
        grad_value_seq = jnp.einsum("kgqs,qkgd->skd", probs_low, grad_seq, preferred_element_type=f32)
        return (grad_query_seq, grad_key_seq, grad_value_seq)

    grad_queries, grad_keys, grad_values = lax.map(
        backward_one, (queries, keys_all, values_all, grad_attended, row_maxes, row_totals)
    )
    grad_kv = jnp.concatenate(
        [
            grad_keys.reshape(seq_count, seq_len, kv_cols),
            grad_values.reshape(seq_count, seq_len, kv_cols),
        ],
        axis=-1,
    )
    kv_sum = grad_kv[:, :ctx_tok]
    for back in range(1, ctx_ranks):
        piece = grad_kv[:, back * ctx_tok : (back + 1) * ctx_tok].astype(bf16)
        kv_sum = kv_sum + lax.ppermute(
            piece, "ctx", [(i + back, i) for i in range(ctx_ranks - back)]
        ).astype(f32)
    grad_query_raw = (
        rotate(grad_queries.reshape(seq_count, ctx_tok, query_heads, HD), cosine, -sine)
        .astype(bf16)
        .reshape(rows, query_heads * HD)
    )
    grad_key_raw = (
        rotate(kv_sum[..., :kv_cols].reshape(seq_count, ctx_tok, key_heads, HD), cosine, -sine)
        .astype(bf16)
        .reshape(rows, kv_cols)
    )
    grad_value_raw = kv_sum[..., kv_cols:].astype(bf16).reshape(rows, kv_cols)
    normed_cols = dp_columns(normed)
    grad_query = ctx_scatter(dot_tn(normed_cols, dp_rows(grad_query_raw)))
    grad_key_value = ctx_scatter(
        dot_tn(normed_cols, dp_rows(jnp.concatenate([grad_key_raw, grad_value_raw], axis=-1)))
    )
    grad_key = grad_key_value[:, :kv_cols]
    grad_value = grad_key_value[:, kv_cols:]
    grad_normed_first = (
        dot_nt(grad_query_raw, query_weight)
        + dot_nt(grad_key_raw, key_weight)
        + dot_nt(grad_value_raw, value_weight)
    ).reshape(seq_count, ctx_tok, width)
    attn_gain_part = jnp.sum(grad_normed_first * unit_first, axis=(0, 1))
    gains = lax.psum(
        jnp.stack([attn_gain_part, mlp_gain_part]), ("dp", "ctx", "tensor")
    )
    gain_rows = width // (lax.axis_size("dp") * ctx_ranks)
    gain_at = (lax.axis_index("dp") * ctx_ranks + ctx_at) * gain_rows
    gains = lax.dynamic_slice_in_dim(gains, gain_at, gain_rows, 1)

    scaled_first = gain_first * sum_share(grad_normed_first)
    unit_share = share_of(unit_first)
    input_grad = share_of(grad_hidden) + share_of(r_first) * (
        scaled_first - unit_share * jnp.mean(scaled_first * unit_share, axis=-1, keepdims=True)
    )
    return (
        block_out,
        input_grad,
        gains[0],
        grad_query,
        grad_key,
        grad_value,
        grad_output,
        gains[1],
        grad_gate,
        grad_up,
        grad_down,
    )


def solution(mesh):
    in_specs = (
        P("dp", "ctx", None),
        P(),
        P(None, "tensor"),
        P(None, "tensor"),
        P(None, "tensor"),
        P("tensor", None),
        P(),
        P(None, "tensor"),
        P(None, "tensor"),
        P("tensor", None),
        P("dp", "ctx", None),
    )
    out_specs = (
        P("dp", ("ctx", "tensor"), None),
        P("dp", ("ctx", "tensor"), None),
        P(("dp", "ctx")),
        P(("dp", "ctx"), "tensor"),
        P(("dp", "ctx"), "tensor"),
        P(("dp", "ctx"), "tensor"),
        P("tensor", ("dp", "ctx")),
        P(("dp", "ctx")),
        P(("dp", "ctx"), "tensor"),
        P(("dp", "ctx"), "tensor"),
        P("tensor", ("dp", "ctx")),
    )
    return jax.shard_map(shards, mesh=mesh, in_specs=in_specs, out_specs=out_specs, check_vma=False)
```

time: 1210 us -> 592 us (0.49)
  waiting for transfers between devices: 859 us -> 247 us
  starting transfers between devices: 1.26 us -> 39.9 us
  matrix products: 154 us -> 126 us
  blocking collectives: 72.8 us -> 52.1 us
  other arithmetic: 37.8 us -> 56.2 us
  local copies, waits for them, and re-layouts: 63.8 us -> 51 us
    reduce_scatter x8 -> x6, waiting for transfers between devices: 502 us -> 13 us  [ctx_scatter(): lax.psum_scatter(block.astype(bf16), 'ctx', scatter_dimension=0, tiled=True)]
    unnamed x17 -> x6, waiting for transfers between devices: 272 us -> 0.1 us
    ppermute x0 -> x32, waiting for transfers between devices: none -> 234 us  [the longest x12 128 us: dp_rows(): lax.ppermute(rows, 'dp', xor_pairs(count, bit))]
    psum x2 -> x0, waiting for transfers between devices: 64 us -> none  [the longest x1 63.4 us: shards(): branch_full = lax.psum(branch_part, 'tensor')]
    psum x1, blocking collectives: 6.94 us -> 52.1 us  [shards(): lax.psum(jnp.stack([attn_gain_part, mlp_gain_part]), ('dp', 'ctx', 'tenso...]
    ppermute x0 -> x32, starting transfers between devices: none -> 39.2 us  [the longest x3 10.9 us: shards(): lax.ppermute(kv_local, 'ctx', [(i, i + back) for i in range(ctx_ranks - b...]
    all_gather x2 -> x0, blocking collectives: 33.3 us -> none  [the longest x1 18 us: shards(): lax.all_gather(values_local, 'ctx', axis=1, tiled=True)]
    unnamed x1 -> x0, blocking collectives: 32.6 us -> none
  transfers between devices with their start and end apart: 14 -> 38, of which waited for: 13 -> 21; matrix products, arithmetic and copies ran while one was open for 10% -> 26% of each run, Pallas kernels for 0% -> 0%
where the time goes in v1:
time: 592 us; the launch traced here: 588 us
  waiting for transfers between devices  247 us (42%)
  matrix products  126 us (21%)
  other arithmetic  56.2 us (9%)
  blocking collectives  52.1 us (9%)
  local copies, waits for them, and re-layouts  51 us (9%)
  starting transfers between devices  39.9 us (7%)
  between operations  15.4 us (3%)
    ppermute x12, waiting for transfers between devices, dp_rows(): lax.ppermute(rows, 'dp', xor_pairs(count, bit))  128 us
    ppermute x5, waiting for transfers between devices, swap_tensor(): return lax.ppermute(values, 'tensor', [(0, 1), (1, 0)])  56.7 us
    psum x1, blocking collectives, shards(): lax.psum(jnp.stack([attn_gain_part, mlp_gain_part]), ('dp', 'ctx', 'tenso...  52.1 us
    dot_general x7, matrix products, dot_nt(): lax.dot_general(left, right, (((1,), (1,)), ((), ())), preferred_element_...  46.6 us
    dot_general x8, matrix products, dot_nn(): lax.dot_general(left, right, (((1,), (0,)), ((), ())), preferred_element_...  36 us
    ppermute x8, waiting for transfers between devices, dp_columns(): lax.ppermute(give, 'dp', xor_pairs(count, bit))  33.3 us
    dot_general x6, matrix products, dot_tn(): lax.dot_general(left, right, (((0,), (0,)), ((), ())), preferred_element_...  28.8 us
    unnamed x124, local copies, waits for them, and re-layouts  23.8 us
  transfers between devices with their start and end apart: 38, of which 21 were waited for; matrix products, arithmetic and copies ran while one was open for 26% of the time, Pallas kernels for 0%

profile of v1, /device:TPU:0, one launch (start us, length us, event | category | flops | bytes accessed | tf_op | source)
XLA Modules:
  0.0 587.9 jit_solution(12576051747239383631)
XLA Ops:
  7.3 3.3 constant_dynamic-slice_fusion.10
  10.6 3.0 collective-permute-start.4
  19.8 6.2 %collective-permute-start.2 = (bf16[2,128,512]{1,2,0:T(8,128)(2,1)}, bf16[2,128,512]{1,2,0:T(8,128)(2,1)}, u32[]{:S(2)}, u32[]{:S(2)}) collective-permute-start(bf16[2,128,512]{1,2,0:T(8,128)(2,1)} %pad_maximum_fusion.16), channel_id=1, source_target_pairs={{0,6},{1,7},{8,14},{9,15},{16,22},{17,23},{24,30},{25,31}} | collective-permute-start | bytes 786440 | tf_op jit(solution)/shard_map/ppermute | solution.py:167
  28.0 2.7 collective-permute-start
  30.7 6.5 %copy.56 = bf16[2048,1024]{0,1:T(8,128)(2,1)} copy(bf16[2048,1024]{1,0:T(8,128)(2,1)} %param.17) | data formatting | bytes 8388608 | tf_op args[2]
  37.2 3.5 fusion.130
  43.5 16.0 %collective-permute-done.4 = bf16[512,2048]{1,0:T(8,128)(2,1)} collective-permute-done((bf16[512,2048]{1,0:T(8,128)(2,1)}, bf16[512,2048]{1,0:T(8,128)(2,1)}, u32[]{:S(2)}, u32[]{:S(2)}) %collective-permute-start.4) | collective-permute-done | bytes 2097184 | tf_op jit(solution)/shard_map/ppermute | solution.py:84
  59.5 8.1 %while.30 = (s32[]{:T(128)}, bf16[2,128,4,4,64]{1,4,3,2,0:T(8,128)(2,1)}, f32[2,4,4,128,1]{3,2,1,4,0:T(4,128)S(1)}, f32[2,4,4,128,1]{3,2,1,4,0:T(4,128)S(1)}, bf...) while((s32[]{:T(128)}, ...), condition=%wide.region_4.5_spmd.clone, body=%wide.region_1.4_spmd.clone.sunk | while | flops 281276416 | bytes 18164904 | solution.py:202
  71.5 3.6 fusion.159
  75.2 2.6 broadcast_select_fusion.1
  77.9 6.3 %collective-permute-done.3 = bf16[256,1024]{0,1:T(8,128)(2,1)S(1)} collective-permute-done((bf16[256,1024]{0,1:T(8,128)(2,1)S(1)}, bf16[256,1024]{0,1:T(8,128)(2,1)S(1)}, u32[]{:S(2)}, u32[]{:S(2)}) %collective-permute-start.3) | collective-permute-done | bytes 524320 | tf_op jit(solution)/shard_map/ppermute | solution.py:84
  88.3 6.2 %fusion.165 = f32[256,4096]{1,0:T(8,128)} fusion(bf16[256,2048]{1,0:T(8,128)(2,1)S(1)} %bitcast.282, bf16[2048,4096]{1,0:T(8,128)(2,1)S(1)} %bitcast.321), kind=kOutput, calls=%fused_computation.265 | convolution fusion | flops 4294967296 | bytes 22020096 | tf_op jit(solution)/shard_map/dot_general | solution.py:39
  94.4 10.6 %fusion.166 = f32[256,4096]{1,0:T(8,128)} fusion(bf16[256,2048]{1,0:T(8,128)(2,1)S(1)} %bitcast.283, bf16[2048,4096]{1,0:T(8,128)(2,1)} %param.23), kind=kOutput, calls=%fused_computation.266 | convolution fusion | flops 4294967296 | bytes 22020096 | tf_op jit(solution)/shard_map/dot_general | solution.py:39
  105.0 13.1 %multiply_convert_fusion = (bf16[256,4096]{1,0:T(8,128)(2,1)}, bf16[256,4096]{1,0:T(8,128)(2,1)}, bf16[256,4096]{1,0:T(8,128)(2,1)}) fusion(f32[256,4096]{1,0:T(8,128)} %fusion.165, f32[256,4096]{1,0:T(8,128)} %fusion.166, bf16[256,2048]{1,0:T(8,128)(2,1)S(1)} %bitcast.285, bf16[4096,2048]{1,0:T(8,128)(2,1)} %param.24), kind=kOutput, calls=%fused_computation.98 | convolution fusion | flops 4310695936 | bytes 32505856 | tf_op jit(solution)/shard_map/dot_general | solution.py:47
  118.1 12.3 %fusion.168 = f32[256,2048]{1,0:T(8,128)} fusion(bf16[256,4096]{1,0:T(8,128)(2,1)} %get-tuple-element.296, bf16[2048,4096]{1,0:T(8,128)(2,1)} %param.22), kind=kOutput, calls=%fused_computation.268 | convolution fusion | flops 4294967296 | bytes 20971520 | tf_op jit(solution)/shard_map/dot_general | solution.py:47
  130.3 13.1 %bitcast_convert_fusion = (bf16[2,128,2048]{2,1,0:T(8,128)(2,1)}, f32[256,2048]{1,0:T(8,128)}) fusion(f32[256,2048]{1,0:T(8,128)} %fusion.168, bf16[256,4096]{1,0:T(8,128)(2,1)} %get-tuple-element.295, bf16[2048,4096]{1,0:T(8,128)(2,1)} %param.23), kind=kOutput, calls=%fused_computation.258 | convolution fusion | flops 4296015872 | bytes 24117248 | tf_op jit(solution)/shard_map/dot_general | solution.py:47
  146.7 21.8 %collective-permute-done.7 = bf16[2,128,2048]{2,1,0:T(8,128)(2,1)} collective-permute-done((bf16[2,128,2048]{2,1,0:T(8,128)(2,1)}, bf16[2,128,2048]{2,1,0:T(8,128)(2,1)}, u32[]{:S(2)}, u32[]{:S(2)}) %collective-permute-start.7) | collective-permute-done | bytes 1048608 | tf_op jit(solution)/shard_map/ppermute | solution.py:84
  168.5 3.6 multiply_reduce_fusion
  172.1 3.6 fusion.161
  178.8 3.4 reshape.283
  182.2 2.6 copy.59
  184.8 17.9 %while.31 = (s32[]{:T(128)}, f32[2,128,4,4,64]{1,4,3,2,0:T(8,128)}, f32[2,512,4,64]{1,3,2,0:T(8,128)}, f32[2,512,4,64]{1,3,2,0:T(8,128)}, bf16[2,512,4,64]{1,3,2...) while((s32[]{:T(128)}, f32[2,128,4,4,64]{1,4,3,2,0:T(8,128)}, ...), condition=%wide.region_9.10_spmd.clone, body=%wide.region_7.9_spmd.clone.sunk | while | flops 681965568 | bytes 66525572 | solution.py:266
  209.3 2.4 constant_dynamic-slice_fusion.6
  213.4 5.2 collective-permute-done.10
  218.6 9.1 %collective-permute-done.9 = bf16[2,128,512]{1,2,0:T(8,128)(2,1)} collective-permute-done((bf16[2,128,512]{1,2,0:T(8,128)(2,1)}, bf16[2,128,512]{1,2,0:T(8,128)(2,1)}, u32[]{:S(2)}, u32[]{:S(2)}) %collective-permute-start.9) | collective-permute-done | bytes 262176 | tf_op jit(solution)/shard_map/ppermute | solution.py:279
  235.2 6.0 %collective-permute-done.16 = bf16[256,512]{0,1:T(8,128)(2,1)} collective-permute-done((bf16[256,512]{0,1:T(8,128)(2,1)}, bf16[256,512]{0,1:T(8,128)(2,1)}, u32[]{:S(2)}, u32[]{:S(2)}) %collective-permute-start.16) | collective-permute-done | bytes 262176 | tf_op jit(solution)/shard_map/ppermute | solution.py:67
  242.3 9.1 %collective-permute-done.20 = bf16[256,1024]{0,1:T(8,128)(2,1)} collective-permute-done((bf16[256,1024]{0,1:T(8,128)(2,1)}, bf16[256,1024]{0,1:T(8,128)(2,1)}, u32[]{:S(2)}, u32[]{:S(2)}) %collective-permute-start.20) | collective-permute-done | bytes 524320 | tf_op jit(solution)/shard_map/ppermute | solution.py:67
  257.0 2.5 convolution_convert_fusion
  259.7 4.8 pad_maximum_fusion.2
  264.7 4.5 collective-permute-done.18
  272.6 3.7 fusion.111
  280.5 12.6 %collective-permute-done.14 = bf16[256,1024]{0,1:T(8,128)(2,1)S(1)} collective-permute-done((bf16[256,1024]{0,1:T(8,128)(2,1)S(1)}, bf16[256,1024]{0,1:T(8,128)(2,1)S(1)}, u32[]{:S(2)}, u32[]{:S(2)}) %collective-permute-start.14) | collective-permute-done | bytes 524320 | tf_op jit(solution)/shard_map/ppermute | solution.py:67
  298.3 10.7 %collective-permute-done.28 = bf16[256,1024]{1,0:T(8,128)(2,1)} collective-permute-done((bf16[256,1024]{1,0:T(8,128)(2,1)}, bf16[256,1024]{1,0:T(8,128)(2,1)}, u32[]{:S(2)}, u32[]{:S(2)}) %collective-permute-start.28) | collective-permute-done | bytes 524320 | tf_op jit(solution)/shard_map/ppermute | solution.py:79
  312.3 8.0 %fusion.80 = bf16[512,4096]{1,0:T(8,128)(2,1)} fusion(bf16[512,4096]{1,0:T(8,128)(2,1)} %collective-permute-done.31, bf16[256,4096]{1,0:T(8,128)(2,1)} %collective-permute-done.30, bf16[256,4096]{1,0:T(8,128)(2,1)S(1)} %copy-done.34, bf16[512,512]{1,0:T(8,128)(2,1)S(1)} %collective-permute-done.29, bf16[512,512]{1,0:T(8,128)(2,1)S(1)} %get-tuple-element.306), kind=kOutput, calls=%fused_computation.88 | convolution fusion | flops 4324327424 | bytes 13631488 | tf_op jit(solution)/shard_map/dot_general | solution.py:43
  321.8 46.5 %collective-permute-done.24 = bf16[256,4096]{1,0:T(8,128)(2,1)S(1)} collective-permute-done((bf16[256,4096]{1,0:T(8,128)(2,1)}, bf16[256,4096]{1,0:T(8,128)(2,1)S(1)}, u32[]{:S(2)}, u32[]{:S(2)}) %collective-permute-start.24) | collective-permute-done | bytes 2097184 | tf_op jit(solution)/shard_map/ppermute | solution.py:67
  372.0 13.0 %collective-permute-done.22 = bf16[256,1024]{1,0:T(8,128)(2,1)S(1)} collective-permute-done((bf16[256,1024]{1,0:T(8,128)(2,1)S(1)}, bf16[256,1024]{1,0:T(8,128)(2,1)S(1)}, u32[]{:S(2)}, u32[]{:S(2)}) %collective-permute-start.22) | collective-permute-done | bytes 524320 | tf_op jit(solution)/shard_map/ppermute | solution.py:79
  387.9 6.2 %fusion.86 = bf16[512,4096]{1,0:T(8,128)(2,1)} fusion(bf16[512,4096]{1,0:T(8,128)(2,1)S(1)} %collective-permute-done.25, bf16[256,4096]{1,0:T(8,128)(2,1)S(1)} %collective-permute-done.24, bf16[256,4096]{1,0:T(8,128)(2,1)S(1)} %copy-done.36, bf16[512,512]{1,0:T(8,128)(2,1)S(1)} %collective-permute-done.23, bf16[512,512]{1,0:T(8,128)(2,1)S(1)} %get-tuple-element.310), kind=kOutput, calls=%fused_computation.90 | convolution fusion | flops 4324327424 | bytes 13631488 | tf_op jit(solution)/shard_map/dot_general | solution.py:43
  395.8 46.5 %collective-permute-done.26 = bf16[256,4096]{1,0:T(8,128)(2,1)S(1)} collective-permute-done((bf16[256,4096]{1,0:T(8,128)(2,1)}, bf16[256,4096]{1,0:T(8,128)(2,1)S(1)}, u32[]{:S(2)}, u32[]{:S(2)}) %collective-permute-start.26) | collective-permute-done | bytes 2097184 | tf_op jit(solution)/shard_map/ppermute | solution.py:67
  444.5 7.1 %collective-permute-done.27 = bf16[512,4096]{1,0:T(8,128)(2,1)S(1)} collective-permute-done((bf16[512,4096]{1,0:T(8,128)(2,1)S(1)}, bf16[512,4096]{1,0:T(8,128)(2,1)S(1)}, u32[]{:S(2)}, u32[]{:S(2)}) %collective-permute-start.27) | collective-permute-done | bytes 4194336 | tf_op jit(solution)/shard_map/ppermute | solution.py:67
  451.7 6.2 %fusion.83 = bf16[512,4096]{1,0:T(8,128)(2,1)} fusion(bf16[512,4096]{1,0:T(8,128)(2,1)S(1)} %collective-permute-done.27, bf16[256,4096]{1,0:T(8,128)(2,1)S(1)} %collective-permute-done.26, bf16[256,4096]{1,0:T(8,128)(2,1)S(1)} %copy-done.35, bf16[512,512]{1,0:T(8,128)(2,1)S(1)} %copy-done.64, bf16[512,512]{1,0:T(8,128)(2,1)S(1)} %copy-done.49), kind=kOutput, calls=%fused_computation.89 | convolution fusion | flops 4324327424 | bytes 13631488 | tf_op jit(solution)/shard_map/dot_general | solution.py:43
  457.9 8.8 %fusion.167 = f32[256,2048]{1,0:T(8,128)S(1)} fusion(bf16[256,4096]{1,0:T(8,128)(2,1)} %get-tuple-element.297, bf16[4096,2048]{1,0:T(8,128)(2,1)} %param.24), kind=kOutput, calls=%fused_computation.267 | convolution fusion | flops 4294967296 | bytes 20971520 | tf_op jit(solution)/shard_map/dot_general | solution.py:39
  470.5 12.7 %collective-permute-done.6 = bf16[2,64,2048]{2,1,0:T(8,128)(2,1)} collective-permute-done((bf16[2,64,2048]{2,1,0:T(8,128)(2,1)}, bf16[2,64,2048]{2,1,0:T(8,128)(2,1)}, u32[]{:S(2)}, u32[]{:S(2)}) %collective-permute-start.6) | collective-permute-done | bytes 524320 | tf_op jit(solution)/shard_map/ppermute | solution.py:84
  485.5 3.7 fusion.160
  496.1 52.1 %psum.7 = f32[2,2048]{1,0:T(2,128)S(1)} all-reduce(f32[2,2048]{1,0:T(2,128)S(1)} %pad_maximum_fusion.20), channel_id=1, replica_groups=mesh['dp'=4,'ctx'=4,'tensor'=2] {'dp','ctx','tensor'}, use_global_device_ids=true, to_apply=%region_13.14 | all-reduce | flops 4096 | bytes 32768 | tf_op jit(solution)/shard_map/psum | solution.py:306
  550.7 3.0 multiply_add_fusion.1
  562.3 2.8 convert_element_type.177
  565.1 13.0 %reduce-scatter.15.cloned.1.call-done = bf16[128,4096]{1,0:T(8,128)(2,1)} async-done(((bf16[512,4096]{1,0:T(8,128)(2,1)}), bf16[128,4096]{1,0:T(8,128)(2,1)}) %reduce-scatter.15.cloned.1.call-update) | async-done | bytes 1048592 | tf_op jit(solution)/shard_map/reduce_scatter | solution.py:116
  578.1 2.8 convert_element_type.179
  (330 shorter events, 125.4 us)
Async XLA Ops:
  7.2 546.5 %reduce-scatter.9.cloned.1.call-start = ((), (), s32[]{:S(2)}) async-start(), calls=%async_computation.7 | async-start | bytes 655360 | tf_op jit(solution)/shard_map/reduce_scatter | solution.py:116
  10.6 48.9 %collective-permute-start.4 = (bf16[512,2048]{1,0:T(8,128)(2,1)}, bf16[512,2048]{1,0:T(8,128)(2,1)}, u32[]{:S(2)}, u32[]{:S(2)}) collective-permute-start(bf16[512,2048]{1,0:T(8,128)(2,1)} %constant_dynamic-slice_fusion.10), channel_id=1, source_target_pairs={{0,1},{1,0},{2,3},{3,2},{4,5},{5,4},{6,7},{7,6},{8,9},{9,8},{10,11... | collective-permute-start | bytes 6291464 | tf_op jit(solution)/shard_map/ppermute | solution.py:84
  14.2 23.0 %copy-start.11 = (bf16[2,128,2048]{2,1,0:T(8,128)(2,1)}, bf16[2,128,2048]{2,1,0:T(8,128)(2,1)S(1)}, u32[]{:S(2)}) copy-start(bf16[2,128,2048]{2,1,0:T(8,128)(2,1)S(1)} %multiply_convert_fusion.4) | copy-start | bytes 3145732
  15.5 25.2 %copy-start.50 = (f32[128,32]{0,1:T(8,128)}, f32[128,32]{0,1:T(8,128)S(1)}, u32[]{:S(2)}) copy-start(f32[128,32]{0,1:T(8,128)S(1)} %get-tuple-element.337) | copy-start | bytes 49156
  19.8 21.3 %collective-permute-start.2 = (bf16[2,128,512]{1,2,0:T(8,128)(2,1)}, bf16[2,128,512]{1,2,0:T(8,128)(2,1)}, u32[]{:S(2)}, u32[]{:S(2)}) collective-permute-start(bf16[2,128,512]{1,2,0:T(8,128)(2,1)} %pad_maximum_fusion.16), channel_id=1, source_target_pairs={{0,6},{1,7},{8,14},{9,15},{16,22},{17,23},{24,30},{25,31}} | collective-permute-start | bytes 786440 | tf_op jit(solution)/shard_map/ppermute | solution.py:167
  26.0 15.1 %collective-permute-start.1 = (bf16[2,128,512]{1,2,0:T(8,128)(2,1)}, bf16[2,128,512]{1,2,0:T(8,128)(2,1)}, u32[]{:S(2)}, u32[]{:S(2)}) collective-permute-start(bf16[2,128,512]{1,2,0:T(8,128)(2,1)} %pad_maximum_fusion.16), channel_id=1, source_target_pairs={{0,4},{2,6},{1,5},{3,7},{8,12},{10,14},{9,13},{11,15},{16,20},{18,... | collective-permute-start | bytes 786440 | tf_op jit(solution)/shard_map/ppermute | solution.py:167
  28.0 14.2 %collective-permute-start = (bf16[2,128,512]{1,2,0:T(8,128)(2,1)}, bf16[2,128,512]{1,2,0:T(8,128)(2,1)}, u32[]{:S(2)}, u32[]{:S(2)}) collective-permute-start(bf16[2,128,512]{1,2,0:T(8,128)(2,1)} %pad_maximum_fusion.16), channel_id=1, source_target_pairs={{0,2},{2,4},{4,6},{1,3},{3,5},{5,7},{8,10},{10,12},{12,14},{9,11},... | collective-permute-start | bytes 786440 | tf_op jit(solution)/shard_map/ppermute | solution.py:167
  59.5 15.7 %collective-permute-start.5 = (bf16[512,2048]{1,0:T(8,128)(2,1)}, bf16[512,2048]{1,0:T(8,128)(2,1)}, u32[]{:S(2)}, u32[]{:S(2)}) collective-permute-start(bf16[512,2048]{1,0:T(8,128)(2,1)} %collective-permute-done.4), channel_id=1, source_target_pairs={{0,8},{8,0},{16,24},{24,16},{1,9},{9,1},{17,25},{25,17},{2,10},{10... | collective-permute-start | bytes 6291464 | tf_op jit(solution)/shard_map/ppermute | solution.py:110
  69.7 14.4 %collective-permute-start.3 = (bf16[256,1024]{0,1:T(8,128)(2,1)S(1)}, bf16[256,1024]{0,1:T(8,128)(2,1)S(1)}, u32[]{:S(2)}, u32[]{:S(2)}) collective-permute-start(bf16[256,1024]{0,1:T(8,128)(2,1)S(1)} %bitcast.294), channel_id=1, source_target_pairs={{0,1},{1,0},{2,3},{3,2},{4,5},{5,4},{6,7},{7,6},{8,9},{9,8},{10,11... | collective-permute-start | bytes 1572872 | tf_op jit(solution)/shard_map/ppermute | solution.py:84
  143.5 25.0 %collective-permute-start.7 = (bf16[2,128,2048]{2,1,0:T(8,128)(2,1)}, bf16[2,128,2048]{2,1,0:T(8,128)(2,1)}, u32[]{:S(2)}, u32[]{:S(2)}) collective-permute-start(bf16[2,128,2048]{2,1,0:T(8,128)(2,1)} %get-tuple-element.338), channel_id=1, source_target_pairs={{0,1},{1,0},{2,3},{3,2},{4,5},{5,4},{6,7},{7,6},{8,9},{9,8},{10,11... | collective-permute-start | bytes 3145736 | tf_op jit(solution)/shard_map/ppermute | solution.py:84
  145.2 114.5 %collective-permute-start.30 = (bf16[256,4096]{1,0:T(8,128)(2,1)}, bf16[256,4096]{1,0:T(8,128)(2,1)}, u32[]{:S(2)}, u32[]{:S(2)}) collective-permute-start(bf16[256,4096]{1,0:T(8,128)(2,1)} %get-tuple-element.297), channel_id=1, source_target_pairs={{0,16},{8,24},{16,0},{24,8},{1,17},{9,25},{17,1},{25,9},{2,18},{10... | collective-permute-start | bytes 6291464 | tf_op jit(solution)/shard_map/ppermute | solution.py:67
  205.3 13.3 %collective-permute-start.10 = (bf16[2,128,512]{1,2,0:T(8,128)(2,1)}, bf16[2,128,512]{1,2,0:T(8,128)(2,1)}, u32[]{:S(2)}, u32[]{:S(2)}) collective-permute-start(bf16[2,128,512]{1,2,0:T(8,128)(2,1)} %get-tuple-element.323), channel_id=1, source_target_pairs={{6,0},{7,1},{14,8},{15,9},{22,16},{23,17},{30,24},{31,25}} | collective-permute-start | bytes 786440 | tf_op jit(solution)/shard_map/ppermute | solution.py:279
  206.6 21.1 %collective-permute-start.9 = (bf16[2,128,512]{1,2,0:T(8,128)(2,1)}, bf16[2,128,512]{1,2,0:T(8,128)(2,1)}, u32[]{:S(2)}, u32[]{:S(2)}) collective-permute-start(bf16[2,128,512]{1,2,0:T(8,128)(2,1)} %get-tuple-element.324), channel_id=1, source_target_pairs={{4,0},{6,2},{5,1},{7,3},{12,8},{14,10},{13,9},{15,11},{20,16},{22,... | collective-permute-start | bytes 786440 | tf_op jit(solution)/shard_map/ppermute | solution.py:279
  207.9 19.8 %collective-permute-start.8 = (bf16[2,128,512]{1,2,0:T(8,128)(2,1)S(1)}, bf16[2,128,512]{1,2,0:T(8,128)(2,1)}, u32[]{:S(2)}, u32[]{:S(2)}) collective-permute-start(bf16[2,128,512]{1,2,0:T(8,128)(2,1)S(1)} %get-tuple-element.322), channel_id=1, source_target_pairs={{2,0},{4,2},{6,4},{3,1},{5,3},{7,5},{10,8},{12,10},{14,12},{11,9},... | collective-permute-start | bytes 786440 | tf_op jit(solution)/shard_map/ppermute | solution.py:279
  209.2 18.4 %copy-start.15 = (f32[2,512,4,64]{1,3,2,0:T(8,128)S(1)}, f32[2,512,4,64]{1,3,2,0:T(8,128)}, u32[]{:S(2)}) copy-start(f32[2,512,4,64]{1,3,2,0:T(8,128)} %get-tuple-element.118) | copy-start | bytes 3145732
  211.7 22.1 %collective-permute-start.12 = (bf16[256,1024]{1,0:T(8,128)(2,1)}, bf16[256,1024]{1,0:T(8,128)(2,1)}, u32[]{:S(2)}, u32[]{:S(2)}) collective-permute-start(bf16[256,1024]{1,0:T(8,128)(2,1)} %get-tuple-element.320), channel_id=1, source_target_pairs={{0,16},{8,24},{16,0},{24,8},{1,17},{9,25},{17,1},{25,9},{2,18},{10... | collective-permute-start | bytes 1572872 | tf_op jit(solution)/shard_map/ppermute | solution.py:79
  231.7 9.5 %collective-permute-start.16 = (bf16[256,512]{0,1:T(8,128)(2,1)}, bf16[256,512]{0,1:T(8,128)(2,1)}, u32[]{:S(2)}, u32[]{:S(2)}) collective-permute-start(bf16[256,512]{0,1:T(8,128)(2,1)} %pad_maximum_fusion.17), channel_id=1, source_target_pairs={{0,16},{8,24},{16,0},{24,8},{1,17},{9,25},{17,1},{25,9},{2,18},{10... | collective-permute-start | bytes 786440 | tf_op jit(solution)/shard_map/ppermute | solution.py:67
  233.4 18.0 %collective-permute-start.20 = (bf16[256,1024]{0,1:T(8,128)(2,1)}, bf16[256,1024]{0,1:T(8,128)(2,1)}, u32[]{:S(2)}, u32[]{:S(2)}) collective-permute-start(bf16[256,1024]{0,1:T(8,128)(2,1)} %bitcast.295), channel_id=1, source_target_pairs={{0,16},{8,24},{16,0},{24,8},{1,17},{9,25},{17,1},{25,9},{2,18},{10... | collective-permute-start | bytes 1572872 | tf_op jit(solution)/shard_map/ppermute | solution.py:67
  235.1 21.2 %copy-start.46 = (bf16[512,512]{1,0:T(8,128)(2,1)}, bf16[512,512]{1,0:T(8,128)(2,1)S(1)}, u32[]{:S(2)}) copy-start(bf16[512,512]{1,0:T(8,128)(2,1)S(1)} %get-tuple-element.318) | copy-start | bytes 1572868
  235.1 21.2 %collective-permute-start.13 = (bf16[512,512]{1,0:T(8,128)(2,1)S(1)}, bf16[512,512]{1,0:T(8,128)(2,1)S(1)}, u32[]{:S(2)}, u32[]{:S(2)}) collective-permute-start(bf16[512,512]{1,0:T(8,128)(2,1)S(1)} %get-tuple-element.319), channel_id=1, source_target_pairs={{0,8},{8,0},{16,24},{24,16},{1,9},{9,1},{17,25},{25,17},{2,10},{10... | collective-permute-start | bytes 1572872 | tf_op jit(solution)/shard_map/ppermute | solution.py:79
  242.2 14.1 %collective-permute-start.17 = (bf16[512,512]{0,1:T(8,128)(2,1)S(1)}, bf16[512,512]{0,1:T(8,128)(2,1)S(1)}, u32[]{:S(2)}, u32[]{:S(2)}) collective-permute-start(bf16[512,512]{0,1:T(8,128)(2,1)S(1)} %pad_maximum_fusion.15), channel_id=1, source_target_pairs={{0,8},{8,0},{16,24},{24,16},{1,9},{9,1},{17,25},{25,17},{2,10},{10... | collective-permute-start | bytes 1572872 | tf_op jit(solution)/shard_map/ppermute | solution.py:67
  253.5 17.8 %collective-permute-start.21 = (bf16[512,1024]{0,1:T(8,128)(2,1)}, bf16[512,1024]{0,1:T(8,128)(2,1)}, u32[]{:S(2)}, u32[]{:S(2)}) collective-permute-start(bf16[512,1024]{0,1:T(8,128)(2,1)} %pad_maximum_fusion.7), channel_id=1, source_target_pairs={{0,8},{8,0},{16,24},{24,16},{1,9},{9,1},{17,25},{25,17},{2,10},{10... | collective-permute-start | bytes 3145736 | tf_op jit(solution)/shard_map/ppermute | solution.py:67
  254.5 14.7 %collective-permute-start.18 = (bf16[256,1024]{1,0:T(8,128)(2,1)}, bf16[256,1024]{1,0:T(8,128)(2,1)}, u32[]{:S(2)}, u32[]{:S(2)}) collective-permute-start(bf16[256,1024]{1,0:T(8,128)(2,1)} %get-tuple-element.316), channel_id=1, source_target_pairs={{0,16},{8,24},{16,0},{24,8},{1,17},{9,25},{17,1},{25,9},{2,18},{10... | collective-permute-start | bytes 1572872 | tf_op jit(solution)/shard_map/ppermute | solution.py:79
  259.6 295.7 %reduce-scatter.11.cloned.1.call-start = ((), (), s32[]{:S(2)}) async-start(), calls=%async_computation.8 | async-start | bytes 1310720 | tf_op jit(solution)/shard_map/reduce_scatter | solution.py:116
  264.4 47.8 %collective-permute-start.31 = (bf16[512,4096]{1,0:T(8,128)(2,1)}, bf16[512,4096]{1,0:T(8,128)(2,1)}, u32[]{:S(2)}, u32[]{:S(2)}) collective-permute-start(bf16[512,4096]{1,0:T(8,128)(2,1)} %pad_maximum_fusion.2), channel_id=1, source_target_pairs={{0,8},{8,0},{16,24},{24,16},{1,9},{9,1},{17,25},{25,17},{2,10},{10... | collective-permute-start | bytes 12582920 | tf_op jit(solution)/shard_map/ppermute | solution.py:67
  270.3 2.3 collective-permute-start.19
  276.3 281.0 %reduce-scatter.7.cloned.1.call-start = ((), (), s32[]{:S(2)}) async-start(), calls=%async_computation.6 | async-start | bytes 1310720 | tf_op jit(solution)/shard_map/reduce_scatter | solution.py:116
  279.0 14.1 %collective-permute-start.14 = (bf16[256,1024]{0,1:T(8,128)(2,1)S(1)}, bf16[256,1024]{0,1:T(8,128)(2,1)S(1)}, u32[]{:S(2)}, u32[]{:S(2)}) collective-permute-start(bf16[256,1024]{0,1:T(8,128)(2,1)S(1)} %bitcast.298), channel_id=1, source_target_pairs={{0,16},{8,24},{16,0},{24,8},{1,17},{9,25},{17,1},{25,9},{2,18},{10... | collective-permute-start | bytes 1572872 | tf_op jit(solution)/shard_map/ppermute | solution.py:67
  293.2 2.7 collective-permute-start.15
  294.4 14.6 %collective-permute-start.28 = (bf16[256,1024]{1,0:T(8,128)(2,1)}, bf16[256,1024]{1,0:T(8,128)(2,1)}, u32[]{:S(2)}, u32[]{:S(2)}) collective-permute-start(bf16[256,1024]{1,0:T(8,128)(2,1)} %get-tuple-element.308), channel_id=1, source_target_pairs={{0,16},{8,24},{16,0},{24,8},{1,17},{9,25},{17,1},{25,9},{2,18},{10... | collective-permute-start | bytes 1572872 | tf_op jit(solution)/shard_map/ppermute | solution.py:79
  298.3 260.8 %reduce-scatter.17.cloned.1.call-start = ((), (), s32[]{:S(2)}) async-start(), calls=%async_computation.11 | async-start | bytes 5242880 | tf_op jit(solution)/shard_map/reduce_scatter | solution.py:116
  310.3 2.0 collective-permute-start.29
  320.3 242.0 %reduce-scatter.13.cloned.1.call-start = ((), (), s32[]{:S(2)}) async-start(), calls=%async_computation.9 | async-start | bytes 5242880 | tf_op jit(solution)/shard_map/reduce_scatter | solution.py:116
  320.4 50.1 %copy-start.20 = (bf16[2,128,2048]{2,1,0:T(8,128)(2,1)S(1)}, bf16[2,128,2048]{2,1,0:T(8,128)(2,1)}, u32[]{:S(2)}) copy-start(bf16[2,128,2048]{2,1,0:T(8,128)(2,1)} %copy-done.19) | copy-start | bytes 3145732
  320.4 47.9 %collective-permute-start.24 = (bf16[256,4096]{1,0:T(8,128)(2,1)}, bf16[256,4096]{1,0:T(8,128)(2,1)S(1)}, u32[]{:S(2)}, u32[]{:S(2)}) collective-permute-start(bf16[256,4096]{1,0:T(8,128)(2,1)} %get-tuple-element.296), channel_id=1, source_target_pairs={{0,16},{8,24},{16,0},{24,8},{1,17},{9,25},{17,1},{25,9},{2,18},{10... | collective-permute-start | bytes 6291464 | tf_op jit(solution)/shard_map/ppermute | solution.py:67
  370.4 16.7 %collective-permute-start.25 = (bf16[512,4096]{1,0:T(8,128)(2,1)S(1)}, bf16[512,4096]{1,0:T(8,128)(2,1)S(1)}, u32[]{:S(2)}, u32[]{:S(2)}) collective-permute-start(bf16[512,4096]{1,0:T(8,128)(2,1)S(1)} %pad_maximum_fusion), channel_id=1, source_target_pairs={{0,8},{8,0},{16,24},{24,16},{1,9},{9,1},{17,25},{25,17},{2,10},{10... | collective-permute-start | bytes 12582920 | tf_op jit(solution)/shard_map/ppermute | solution.py:67
  370.6 14.4 %collective-permute-start.22 = (bf16[256,1024]{1,0:T(8,128)(2,1)S(1)}, bf16[256,1024]{1,0:T(8,128)(2,1)S(1)}, u32[]{:S(2)}, u32[]{:S(2)}) collective-permute-start(bf16[256,1024]{1,0:T(8,128)(2,1)S(1)} %get-tuple-element.312), channel_id=1, source_target_pairs={{0,16},{8,24},{16,0},{24,8},{1,17},{9,25},{17,1},{25,9},{2,18},{10... | collective-permute-start | bytes 1572872 | tf_op jit(solution)/shard_map/ppermute | solution.py:79
  385.1 2.0 collective-permute-start.23
  394.1 184.0 %reduce-scatter.15.cloned.1.call-start = ((), (), s32[]{:S(2)}) async-start(), calls=%async_computation.10 | async-start | bytes 5242880 | tf_op jit(solution)/shard_map/reduce_scatter | solution.py:116
  394.4 57.3 %copy-start.35 = (bf16[256,4096]{1,0:T(8,128)(2,1)S(1)}, bf16[256,4096]{1,0:T(8,128)(2,1)}, u32[]{:S(2)}) copy-start(bf16[256,4096]{1,0:T(8,128)(2,1)} %get-tuple-element.295) | copy-start | bytes 6291460
  394.4 57.3 %copy-start.49 = (bf16[512,512]{1,0:T(8,128)(2,1)S(1)}, bf16[512,512]{1,0:T(8,128)(2,1)}, u32[]{:S(2)}) copy-start(bf16[512,512]{1,0:T(8,128)(2,1)} %copy-done.48) | copy-start | bytes 1572868
  394.4 57.3 %copy-start.64 = (bf16[512,512]{1,0:T(8,128)(2,1)S(1)}, bf16[512,512]{1,0:T(8,128)(2,1)}, u32[]{:S(2)}) copy-start(bf16[512,512]{1,0:T(8,128)(2,1)} %copy-done.63) | copy-start | bytes 1572868
  394.4 47.9 %collective-permute-start.26 = (bf16[256,4096]{1,0:T(8,128)(2,1)}, bf16[256,4096]{1,0:T(8,128)(2,1)S(1)}, u32[]{:S(2)}, u32[]{:S(2)}) collective-permute-start(bf16[256,4096]{1,0:T(8,128)(2,1)} %get-tuple-element.295), channel_id=1, source_target_pairs={{0,16},{8,24},{16,0},{24,8},{1,17},{9,25},{17,1},{25,9},{2,18},{10... | collective-permute-start | bytes 6291464 | tf_op jit(solution)/shard_map/ppermute | solution.py:67
  444.4 7.2 %collective-permute-start.27 = (bf16[512,4096]{1,0:T(8,128)(2,1)S(1)}, bf16[512,4096]{1,0:T(8,128)(2,1)S(1)}, u32[]{:S(2)}, u32[]{:S(2)}) collective-permute-start(bf16[512,4096]{1,0:T(8,128)(2,1)S(1)} %pad_maximum_fusion.1), channel_id=1, source_target_pairs={{0,8},{8,0},{16,24},{24,16},{1,9},{9,1},{17,25},{25,17},{2,10},{10... | collective-permute-start | bytes 12582920 | tf_op jit(solution)/shard_map/ppermute | solution.py:67
  468.9 14.3 %collective-permute-start.6 = (bf16[2,64,2048]{2,1,0:T(8,128)(2,1)}, bf16[2,64,2048]{2,1,0:T(8,128)(2,1)}, u32[]{:S(2)}, u32[]{:S(2)}) collective-permute-start(bf16[2,64,2048]{2,1,0:T(8,128)(2,1)} %dynamic-slice_convert_fusion.1), channel_id=1, source_target_pairs={{0,1},{1,0},{2,3},{3,2},{4,5},{5,4},{6,7},{7,6},{8,9},{9,8},{10,11... | collective-permute-start | bytes 1572872 | tf_op jit(solution)/shard_map/ppermute | solution.py:84
  490.4 58.3 %copy-start.55 = (f32[2048]{0:T(1024)S(1)}, f32[2048]{0:T(1024)}, u32[]{:S(2)}) copy-start(f32[2048]{0:T(1024)} %copy-done.54) | copy-start | bytes 24580
  494.5 56.2 %copy-start.10 = (f32[256,2048]{1,0:T(8,128)S(1)}, f32[256,2048]{1,0:T(8,128)}, u32[]{:S(2)}) copy-start(f32[256,2048]{1,0:T(8,128)} %copy-done.9) | copy-start | bytes 6291460
  494.5 54.2 %collective-permute-start.11 = (bf16[2,64,2048]{2,1,0:T(8,128)(2,1)}, bf16[2,64,2048]{2,1,0:T(8,128)(2,1)}, u32[]{:S(2)}, u32[]{:S(2)}) collective-permute-start(bf16[2,64,2048]{2,1,0:T(8,128)(2,1)} %dynamic-slice_convert_fusion), channel_id=1, source_target_pairs={{0,1},{1,0},{2,3},{3,2},{4,5},{5,4},{6,7},{7,6},{8,9},{9,8},{10,11... | collective-permute-start | bytes 1572872 | tf_op jit(solution)/shard_map/ppermute | solution.py:84
  (70 other events, 402.0 us)
Sparse Core Ops, SparseCore 0:
  259.7 24.7 reduce-scatter.8
  286.8 25.6 reduce-scatter.10
  314.7 25.7 reduce-scatter.6
  342.7 75.2 reduce-scatter.16
  420.2 77.2 reduce-scatter.12
  499.7 78.3 reduce-scatter.14
